TPU v7x, 32 devices: a 4x4x1 block of a 4x4x8 slice. The times are simulated.
32 devices in a mesh: rep: 2 (over z, core), dp: 16 (over x, y).
Axes of the slice: x: 4, y: 4, z: 1, core: 2. Of those that a mesh axis runs over, the one named last changes fastest.
The devices are a block of a 4x4x8 slice.
Arguments:
- a: bfloat16 [32, 4, 4096, 640], P(('rep', 'dp')), parts along dimension 0
- g: bfloat16 [32, 4, 4096, 2560], P(('rep', 'dp')), parts along dimension 0
Outputs:
- output: bfloat16 [8, 640, 2560], P('rep'), parts along dimension 0
There are 2 independent parts. A program takes and returns all parts, laid end to end along the dimension named above; each array names one.
All inputs are finite; a program needn't handle non-finite values.
Results may differ from a plain program's by a relative error of at most 0.012.
Values are sent between devices in bfloat16 or wider.
A program may use at most 768 MiB of HBM per device.

v0:
```python
import jax
import jax.numpy as jnp


def solution(mesh):
    groups = mesh.shape["rep"]

    def step(a, g):
        a, g = (t.reshape(groups, -1, *t.shape[1:]) for t in (a, g))
        sums = jnp.einsum("rsntd,rsntf->rndf", a, g, preferred_element_type=jnp.float32)
        return sums.astype(jnp.bfloat16).reshape(-1, *sums.shape[2:])

    return step
```

profile of v0, /device:TPU:97, one launch (start us, length us, event | category | flops | bytes accessed | tf_op | source)
XLA Modules:
  0.0 629.5 jit_solution(3564820634892567940)
XLA Ops:
  0.0 64.2 %fusion.3 = f32[1,4,640,2560]{3,2,1,0:T(8,128)} fusion(bf16[1,4,4096,2560]{3,2,1,0:T(8,128)(2,1)} %param.1, bf16[1,4,4096,640]{3,2,1,0:T(8,128)(2,1)} %param), kind=kOutput, calls=%fused_computation.4 | convolution fusion | flops 53687091200 | bytes 131072000 | tf_op jit(solution)/rsntd,rsntf->rndf/dot_general | solution.py:10
  64.2 565.3 %all-reduce.2 = bf16[1,4,640,2560]{3,2,1,0:T(8,128)(2,1)} all-reduce(f32[1,4,640,2560]{3,2,1,0:T(8,128)} %fusion.3), channel_id=1, replica_groups=[2,16]<=[32], use_global_device_ids=true, to_apply=%add.clone | all-reduce | flops 6553600 | bytes 39321600 | tf_op jit(solution)/rsntd,rsntf->rndf/dot_general | solution.py:10
where the time goes:
time: 630 us
  blocking collectives  565 us (90%)
  matrix products  64.2 us (10%)
    dot_general x1, blocking collectives, step(): jnp.einsum('rsntd,rsntf->rndf', a, g, preferred_element_type=jnp.float32)  565 us
    dot_general x1, matrix products, step(): jnp.einsum('rsntd,rsntf->rndf', a, g, preferred_element_type=jnp.float32)  64.2 us

commit v1 on v0

v1 whole, which is shorter than its diff:
```python
import jax
import jax.numpy as jnp
from jax import lax
from jax.sharding import PartitionSpec as P


def solution(mesh):
    def body(a, g):
        outs = []
        for n in range(a.shape[1]):
            term = lax.dot_general(a[0, n], g[0, n], (((0,), (0,)), ((), ())), preferred_element_type=jnp.float32)
            term = term.astype(jnp.bfloat16)
            if outs:
                term, outs[-1] = lax.optimization_barrier((term, outs[-1]))
            outs.append(lax.psum(term, "dp"))
        return jnp.stack(outs)

    spec = P(("rep", "dp"), None, None, None)
    return jax.shard_map(body, mesh=mesh, in_specs=(spec, spec), out_specs=P("rep", None, None), check_vma=False)
```

time: 630 us -> 398 us (0.63)
  blocking collectives: 565 us -> 0 us
  waiting for transfers between devices: 0 us -> 290 us
  matrix products: 64.2 us -> 83.5 us
  between operations: 0.01 us -> 13.2 us
  other arithmetic: 0 us -> 9.82 us
    dot_general x1 -> x0, blocking collectives: 565 us -> none  [step(): jnp.einsum('rsntd,rsntf->rndf', a, g, preferred_element_type=jnp.float32)]
    psum x0 -> x4, waiting for transfers between devices: none -> 290 us  [body(): outs.append(lax.psum(term, 'dp'))]
    dot_general x1 -> x4, matrix products: 64.2 us -> 83.5 us  [body(): lax.dot_general(a[0, n], g[0, n], (((0,), (0,)), ((), ())), preferred_ele...]
    another operation x0 -> x1, other arithmetic: none -> 9.82 us  [body(): return jnp.stack(outs)]
  transfers between devices with their start and end apart: 0 -> 4, of which waited for: 0 -> 4; matrix products, arithmetic and copies ran while one was open for 0% -> 16% of each run, Pallas kernels for 0% -> 0%
where the time goes in v1:
time: 398 us
  waiting for transfers between devices  290 us (73%)
  matrix products  83.5 us (21%)
  between operations  13.2 us (3%)
  other arithmetic  9.82 us (2%)
    psum x4, waiting for transfers between devices, body(): outs.append(lax.psum(term, 'dp'))  290 us
    dot_general x4, matrix products, body(): lax.dot_general(a[0, n], g[0, n], (((0,), (0,)), ((), ())), preferred_ele...  83.5 us
    another operation x1, other arithmetic, body(): return jnp.stack(outs)  9.82 us
  transfers between devices with their start and end apart: 4, of which 4 were waited for; matrix products, arithmetic and copies ran while one was open for 16% of the time, Pallas kernels for 0%

profile of v1, /device:TPU:97, one launch (start us, length us, event | category | flops | bytes accessed | tf_op | source)
XLA Modules:
  0.0 397.5 jit_solution(6564063610759199119)
XLA Ops:
  6.5 0.0 all-reduce.5.cloned.1.call-start
  6.6 20.9 %fusion.25 = bf16[640,2560]{1,0:T(8,128)(2,1)} fusion(bf16[1,4,4096,2560]{3,2,1,0:T(8,128)(2,1)} %param.3, bf16[1,4,4096,640]{3,2,1,0:T(8,128)(2,1)} %param.2), kind=kOutput, calls=%fused_computation.22 | convolution fusion | flops 13423411200 | bytes 29491200 | tf_op jit(solution)/shard_map/dot_general | solution.py:11
  27.4 0.1 all-reduce.5.cloned.1.call-update
  27.5 0.2 all-reduce.7.cloned.1.call-start
  27.8 20.8 %fusion.20 = bf16[640,2560]{1,0:T(8,128)(2,1)} fusion(bf16[1,4,4096,2560]{3,2,1,0:T(8,128)(2,1)} %param.3, bf16[1,4,4096,640]{3,2,1,0:T(8,128)(2,1)} %param.2), kind=kOutput, calls=%fused_computation.21 | convolution fusion | flops 13423411200 | bytes 29491200 | tf_op jit(solution)/shard_map/dot_general | solution.py:11
  48.5 68.4 %all-reduce.5.cloned.1.call-done = bf16[640,2560]{1,0:T(8,128)(2,1)} async-done(((bf16[640,2560]{1,0:T(8,128)(2,1)}), bf16[640,2560]{1,0:T(8,128)(2,1)}) %all-reduce.5.cloned.1.call-update) | async-done | bytes 3276816 | tf_op jit(solution)/shard_map/psum | solution.py:15
  116.9 0.1 all-reduce.7.cloned.1.call-update
  117.0 0.3 all-reduce.9.cloned.1.call-start
  117.3 20.9 %fusion.30 = bf16[640,2560]{1,0:T(8,128)(2,1)} fusion(bf16[1,4,4096,2560]{3,2,1,0:T(8,128)(2,1)} %param.3, bf16[1,4,4096,640]{3,2,1,0:T(8,128)(2,1)} %param.2), kind=kOutput, calls=%fused_computation.23 | convolution fusion | flops 13423411200 | bytes 29491200 | tf_op jit(solution)/shard_map/dot_general | solution.py:11
  138.2 66.9 %all-reduce.7.cloned.1.call-done = bf16[640,2560]{1,0:T(8,128)(2,1)} async-done(((bf16[640,2560]{1,0:T(8,128)(2,1)}), bf16[640,2560]{1,0:T(8,128)(2,1)}) %all-reduce.7.cloned.1.call-update) | async-done | bytes 3276816 | tf_op jit(solution)/shard_map/psum | solution.py:15
  205.1 0.1 all-reduce.9.cloned.1.call-update
  205.1 0.0 copy-start
  205.1 0.3 all-reduce.11.cloned.1.call-start
  205.5 20.9 %fusion.35 = bf16[640,2560]{1,0:T(8,128)(2,1)} fusion(bf16[1,4,4096,2560]{3,2,1,0:T(8,128)(2,1)} %param.3, bf16[1,4,4096,640]{3,2,1,0:T(8,128)(2,1)} %param.2), kind=kOutput, calls=%fused_computation.24 | convolution fusion | flops 13423411200 | bytes 29491200 | tf_op jit(solution)/shard_map/dot_general | solution.py:11
  226.4 66.8 %all-reduce.9.cloned.1.call-done = bf16[640,2560]{1,0:T(8,128)(2,1)} async-done(((bf16[640,2560]{1,0:T(8,128)(2,1)}), bf16[640,2560]{1,0:T(8,128)(2,1)}) %all-reduce.9.cloned.1.call-update) | async-done | bytes 3276816 | tf_op jit(solution)/shard_map/psum | solution.py:15
  293.2 0.1 all-reduce.11.cloned.1.call-update
  293.3 87.9 %all-reduce.11.cloned.1.call-done = bf16[1,640,2560]{2,1,0:T(8,128)(2,1)} async-done(((bf16[1,640,2560]{2,1,0:T(8,128)(2,1)}), bf16[1,640,2560]{2,1,0:T(8,128)(2,1)}) %all-reduce.11.cloned.1.call-update) | async-done | bytes 3276816 | tf_op jit(solution)/shard_map/psum | solution.py:15
  381.2 0.0 copy-done
  381.2 9.8 %pad_maximum_fusion = bf16[4,640,2560]{2,1,0:T(8,128)(2,1)} fusion(bf16[1,640,2560]{2,1,0:T(8,128)(2,1)} %all-reduce.11.cloned.1.call-done, bf16[1,640,2560]{2,1,0:T(8,128)(2,1)} %bitcast.46, bf16[1,640,2560]{2,1,0:T(8,128)(2,1)} %bitcast.45, bf16[1,640,2560]{2,1,0:T(8,128)(2,1)S(1)} %bitcast.44), kind=kLoop, calls=%fused_computation.12 | loop fusion | flops 19660800 | bytes 26214400 | tf_op jit(solution)/shard_map/stack | solution.py:16
Async XLA Ops:
  6.5 110.4 %all-reduce.5.cloned.1.call-start = ((), (), s32[]{:S(2)}) async-start(), calls=%async_computation | async-start | bytes 6553600 | tf_op jit(solution)/shard_map/psum | solution.py:15
  27.5 177.6 %all-reduce.7.cloned.1.call-start = ((), (), s32[]{:S(2)}) async-start(), calls=%async_computation.1 | async-start | bytes 6553600 | tf_op jit(solution)/shard_map/psum | solution.py:15
  117.0 176.2 %all-reduce.9.cloned.1.call-start = ((), (), s32[]{:S(2)}) async-start(), calls=%async_computation.2 | async-start | bytes 6553600 | tf_op jit(solution)/shard_map/psum | solution.py:15
  205.1 176.0 %copy-start = (bf16[640,2560]{1,0:T(8,128)(2,1)S(1)}, bf16[640,2560]{1,0:T(8,128)(2,1)}, u32[]{:S(2)}) copy-start(bf16[640,2560]{1,0:T(8,128)(2,1)} %all-reduce.5.cloned.1.call-done) | copy-start | bytes 9830404
  205.1 176.0 %all-reduce.11.cloned.1.call-start = ((), (), s32[]{:S(2)}) async-start(), calls=%async_computation.3 | async-start | bytes 6553600 | tf_op jit(solution)/shard_map/psum | solution.py:15
Sparse Core Ops, SparseCore 0:
  27.6 89.2 all-reduce.4
  120.4 84.6 all-reduce.6
  208.5 84.6 all-reduce.8
  296.5 84.5 all-reduce.10

commit v2 on v1

v2 whole, which is shorter than its diff:
```python
import functools
import math

import jax
import jax.numpy as jnp
from jax import lax
from jax.experimental import pallas as pl
from jax.experimental.pallas import tpu as pltpu
from jax.sharding import PartitionSpec as P

LANES = 128
SLOTS = 4
PIECES = 4
G_SLOTS = 3
HOLD = 3


def kernel(side, a_hbm, g_hbm, out, a_buf, g_buf, acc, part, mine, *rest):
    send_bufs, recv_bufs = rest[:4], rest[4:8]
    a_sem, g_sem, send_sem, recv_sem = rest[8:]
    matrices, tokens, rows = a_hbm.shape[1:]
    width = side * LANES
    per_matrix = g_hbm.shape[3] // width
    chunks = matrices * per_matrix
    half1, rows2 = rows // 2, rows // side
    half2 = rows2 // 2
    me = lax.axis_index("dp")
    x, y = me // side, me % side
    bf16, f32 = jnp.bfloat16, jnp.float32

    class Chunk:
        def __init__(self, c):
            odd = c % 2
            self.c, self.slot = c, c % SLOTS
            self.matrix = c // per_matrix
            self.column = (c % per_matrix) * width
            self.p = x * (1 - odd) + y * odd
            self.q = y * (1 - odd) + x * odd
            self.stride1 = side * (1 - odd) + odd
            self.stride2 = side * odd + 1 - odd

        def first(self, d):
            return (self.p + d + side) % side * self.stride1 + self.q * self.stride2

        def second(self, d):
            return self.p * self.stride1 + (self.q + d + side) % side * self.stride2

        def term(self, d, half):
            s = (self.p + d + side) % side
            lanes = pl.ds(pl.multiple_of(s * LANES, LANES), LANES)
            return acc[self.c % 2, half * half1 : (half + 1) * half1, lanes]

        def sub(self, d, half):
            s = (self.q + d + side) % side
            return part[self.slot, pl.ds(pl.multiple_of(s * rows2 + half * half2, half2), half2), :]

        def block(self, d1, start, size):
            s = (self.p + d1 + side) % side
            lanes = pl.ds(pl.multiple_of(self.column + s * LANES, LANES), LANES)
            return out.at[self.matrix, pl.ds(pl.multiple_of(start, 16), size), lanes]

        def copy(self, stage, way):
            to = 1 - 2 * way
            if stage < 4:
                src, dst = send_bufs[stage].at[self.slot, way], recv_bufs[stage].at[self.slot, way]
                device = self.first(to) if stage < 2 else self.second(to)
            elif stage == 4:
                src = dst = self.block(0, self.q * rows2, rows2)
                device = self.second(to)
            elif stage == 5:
                src = dst = self.block(0, (self.q - to + side) % side * rows2 + way * half2, half2)
                device = self.second(to)
            elif stage == 6:
                src = dst = self.block(0, 0, rows)
                device = self.first(to)
            else:
                src = dst = self.block(-to, way * half1, half1)
                device = self.first(to)
            return pltpu.make_async_remote_copy(
                src_ref=src,
                dst_ref=dst,
                send_sem=send_sem.at[stage, way, self.slot],
                recv_sem=recv_sem.at[stage, way, self.slot],
                device_id={"dp": device},
                device_id_type=pl.DeviceIdType.MESH,
            )

        def send(self, stage):
            for way in range(2):
                self.copy(stage, way).start()

        def received(self, stage):
            for way in range(2):
                self.copy(stage, way).wait_recv()

        def sent(self, stage):
            for way in range(2):
                self.copy(stage, way).wait_send()

    def a_copies(n):
        depth = tokens // PIECES
        for i in range(PIECES):
            piece = pl.ds(i * depth, depth)
            yield pltpu.make_async_copy(a_hbm.at[0, n, piece, :], a_buf.at[n % 2, piece, :], a_sem.at[n % 2, i])

    def g_copies(c):
        depth = tokens // PIECES
        lanes = pl.ds(pl.multiple_of(c % per_matrix * width, width), width)
        for i in range(PIECES):
            piece = pl.ds(i * depth, depth)
            yield pltpu.make_async_copy(
                g_hbm.at[0, c // per_matrix, piece, lanes], g_buf.at[c % G_SLOTS, piece, :], g_sem.at[c % G_SLOTS, i]
            )

    def multiply(c):
        k = Chunk(c)

        @pl.when(c % per_matrix == 0)
        def _():
            for copy in a_copies(k.matrix):
                copy.wait()

            @pl.when(k.matrix + 1 < matrices)
            def _():
                for copy in a_copies(k.matrix + 1):
                    copy.start()

        for copy in g_copies(c):
            copy.wait()

        @pl.when(c + 2 < chunks)
        def _():
            for copy in g_copies(c + 2):
                copy.start()

        acc[c % 2] = lax.dot_general(
            a_buf[k.matrix % 2], g_buf[c % G_SLOTS], (((0,), (0,)), ((), ())), preferred_element_type=f32
        )
        buf = send_bufs[0]
        buf[k.slot, 0, :half1] = k.term(2, 0).astype(bf16)
        buf[k.slot, 0, half1:] = k.term(1, 1).astype(bf16)
        buf[k.slot, 1, :half1] = k.term(-1, 0).astype(bf16)
        buf[k.slot, 1, half1:] = k.term(2, 1).astype(bf16)
        k.send(0)

    def relay1(c):
        k = Chunk(c)
        k.received(0)
        got, buf = recv_bufs[0], send_bufs[1]
        buf[k.slot, 0] = (k.term(1, 0) + got[k.slot, 0, :half1].astype(f32)).astype(bf16)
        buf[k.slot, 1] = (k.term(-1, 1) + got[k.slot, 1, half1:].astype(f32)).astype(bf16)
        k.send(1)
        part[k.slot, :half1] = k.term(0, 0) + got[k.slot, 1, :half1].astype(f32)
        part[k.slot, half1:] = k.term(0, 1) + got[k.slot, 0, half1:].astype(f32)

    def shard1(c):
        k = Chunk(c)
        k.received(1)
        got = recv_bufs[1]
        part[k.slot, :half1] += got[k.slot, 0].astype(f32)
        part[k.slot, half1:] += got[k.slot, 1].astype(f32)
        buf = send_bufs[2]
        buf[k.slot, 0, :half2] = k.sub(2, 0).astype(bf16)
        buf[k.slot, 0, half2:] = k.sub(1, 1).astype(bf16)
        buf[k.slot, 1, :half2] = k.sub(-1, 0).astype(bf16)
        buf[k.slot, 1, half2:] = k.sub(2, 1).astype(bf16)
        k.send(2)

    def relay2(c):
        k = Chunk(c)
        k.received(2)
        got, buf = recv_bufs[2], send_bufs[3]
        buf[k.slot, 0] = (k.sub(1, 0) + got[k.slot, 0, :half2].astype(f32)).astype(bf16)
        buf[k.slot, 1] = (k.sub(-1, 1) + got[k.slot, 1, half2:].astype(f32)).astype(bf16)
        k.send(3)
        mine[k.slot, :half2] = k.sub(0, 0) + got[k.slot, 1, :half2].astype(f32)
        mine[k.slot, half2:] = k.sub(0, 1) + got[k.slot, 0, half2:].astype(f32)

    def shard2(c):
        k = Chunk(c)
        k.received(3)
        got = recv_bufs[3]
        low = mine[k.slot, :half2] + got[k.slot, 0].astype(f32)
        high = mine[k.slot, half2:] + got[k.slot, 1].astype(f32)
        k.block(0, k.q * rows2, half2)[...] = low.astype(bf16)
        k.block(0, k.q * rows2 + half2, half2)[...] = high.astype(bf16)
        k.send(4)

    def gather2(c):
        k = Chunk(c)
        k.received(4)
        k.send(5)

    def gathered2(c):
        Chunk(c).received(5)

    def gather1(c):
        Chunk(c).send(6)

    def relay_gather1(c):
        k = Chunk(c)
        k.received(6)
        k.send(7)

    def gathered1(c):
        Chunk(c).received(7)

    sends = [0, 1, 2, 3, 4, 5, 6 + HOLD, 7 + HOLD]
    steps = list(zip(sends, (multiply, relay1, shard1, relay2, shard2, gather2, gather1, relay_gather1)))
    steps += [(6, gathered2), (8 + HOLD, gathered1)]
    steps.sort(key=lambda step: step[0])
    for stage, lag in enumerate(sends):
        steps.append((lag + 2, functools.partial(lambda stage, c: Chunk(c).sent(stage), stage)))

    barrier = pltpu.get_barrier_semaphore()
    here = Chunk(0)
    for copy in (*a_copies(0), *g_copies(0), *g_copies(1)):
        copy.start()
    for to in (1, -1):
        for device in (here.first(to), here.second(to)):
            pl.semaphore_signal(barrier, inc=1, device_id={"dp": device}, device_id_type=pl.DeviceIdType.MESH)
    pl.semaphore_wait(barrier, 4)

    def turn(t, carry):
        for lag, do in steps:
            @pl.when((t >= lag) & (t < lag + chunks))
            def _(lag=lag, do=do):
                do(t - lag)
        return carry

    lax.fori_loop(0, chunks + max(lag for lag, _ in steps), turn, 0)


def write(sums, out, sem):
    matrices, rows = sums.shape[:2]
    size = rows // PIECES
    copies = [
        pltpu.make_async_copy(
            sums.at[n, i * size : (i + 1) * size], out.at[n, i * size : (i + 1) * size], sem.at[n, i]
        )
        for n in range(matrices)
        for i in range(PIECES)
    ]
    for copy in copies:
        copy.start()
    for copy in copies:
        copy.wait()


def solution(mesh):
    side = math.isqrt(mesh.shape["dp"])

    def body(a, g):
        matrices, tokens, rows = a.shape[1:]
        columns = g.shape[3]
        width = side * LANES
        sizes = (rows, rows // 2, rows // side, rows // side // 2)
        messages = [pltpu.VMEM((SLOTS, 2, size, LANES), jnp.bfloat16) for size in sizes]
        sums = pl.pallas_call(
            functools.partial(kernel, side),
            name="gradient_sums",
            out_shape=pltpu.VMEM((matrices, rows, columns), jnp.bfloat16),
            in_specs=[pl.BlockSpec(memory_space=pl.ANY)] * 2,
            out_specs=pl.BlockSpec(memory_space=pltpu.VMEM),
            scratch_shapes=[
                pltpu.VMEM((2, tokens, rows), jnp.bfloat16),
                pltpu.VMEM((G_SLOTS, tokens, width), jnp.bfloat16),
                pltpu.VMEM((2, rows, width), jnp.float32),
                pltpu.VMEM((SLOTS, rows, LANES), jnp.float32),
                pltpu.VMEM((SLOTS, rows // side, LANES), jnp.float32),
                *messages,
                *messages,
                pltpu.SemaphoreType.DMA((2, PIECES)),
                pltpu.SemaphoreType.DMA((G_SLOTS, PIECES)),
                pltpu.SemaphoreType.DMA((8, 2, SLOTS)),
                pltpu.SemaphoreType.DMA((8, 2, SLOTS)),
            ],
            compiler_params=pltpu.CompilerParams(
                collective_id=0, has_side_effects=True, vmem_limit_bytes=50 << 20
            ),
        )(a, g)
        return pl.pallas_call(
            write,
            name="write_sums",
            out_shape=jax.ShapeDtypeStruct(sums.shape, sums.dtype),
            in_specs=[pl.BlockSpec(memory_space=pltpu.VMEM)],
            out_specs=pl.BlockSpec(memory_space=pl.ANY),
            scratch_shapes=[pltpu.SemaphoreType.DMA((matrices, PIECES))],
            compiler_params=pltpu.CompilerParams(vmem_limit_bytes=1 << 20),
        )(sums)

    spec = P(("rep", "dp"), None, None, None)
    return jax.shard_map(body, mesh=mesh, in_specs=(spec, spec), out_specs=P("rep", None, None), check_vma=False)
```

time: 398 us -> 175 us (0.44)
  the two profiles are of different devices: /device:TPU:97 before, /device:TPU:96 now
where the time goes in v2:
time: 175 us
  Pallas kernels  175 us (100%)
    pallas_call x1, Pallas kernels, body(): pl.pallas_call(functools.partial(kernel, side), name='gradient_sums', out...  170 us
    pallas_call x1, Pallas kernels, body(): pl.pallas_call(write, name='write_sums', out_shape=jax.ShapeDtypeStruct(s...  4.87 us

profile of v2, /device:TPU:96, one launch (start us, length us, event | category | flops | bytes accessed | tf_op | source)
XLA Modules:
  0.0 175.3 jit_solution(6069053927677643104)
XLA Ops:
  0.0 170.4 %gradient_sums.1.sums = bf16[4,640,2560]{2,1,0:T(8,128)(2,1)S(1)} custom-call(bf16[1,4,4096,640]{3,2,1,0:T(8,128)(2,1)} %a_hbm.1, bf16[1,4,4096,2560]{3,2,1,0:T(8,128)(2,1)} %g_hbm.1), custom_call_target="tpu_custom_call" | custom-call | tf_op jit(solution)/shard_map/gradient_sums/pallas_call | solution.py:259
  170.4 4.9 %write_sums.1 = bf16[4,640,2560]{2,1,0:T(8,128)(2,1)} custom-call(bf16[4,640,2560]{2,1,0:T(8,128)(2,1)S(1)} %gradient_sums.1.sums), custom_call_target="tpu_custom_call" | custom-call | tf_op jit(solution)/shard_map/write_sums/pallas_call | solution.py:282

commit v3 on v2

--- a/solution.py
+++ b/solution.py
@@ -10,9 +10,9 @@
 
 LANES = 128
 SLOTS = 4
+SEMS = 8
 PIECES = 4
 G_SLOTS = 3
-HOLD = 3
 
 
 def kernel(side, a_hbm, g_hbm, out, a_buf, g_buf, acc, part, mine, *rest):
@@ -24,14 +24,14 @@
     chunks = matrices * per_matrix
     half1, rows2 = rows // 2, rows // side
     half2 = rows2 // 2
-    me = lax.axis_index("dp")
+    me, swap = lax.axis_index("dp"), lax.axis_index("rep") % 2
     x, y = me // side, me % side
     bf16, f32 = jnp.bfloat16, jnp.float32
 
     class Chunk:
         def __init__(self, c):
-            odd = c % 2
-            self.c, self.slot = c, c % SLOTS
+            odd = (c + swap) % 2
+            self.c, self.slot, self.sem = c, c % SLOTS, c % SEMS
             self.matrix = c // per_matrix
             self.column = (c % per_matrix) * width
             self.p = x * (1 - odd) + y * odd
@@ -79,8 +79,8 @@
             return pltpu.make_async_remote_copy(
                 src_ref=src,
                 dst_ref=dst,
-                send_sem=send_sem.at[stage, way, self.slot],
-                recv_sem=recv_sem.at[stage, way, self.slot],
+                send_sem=send_sem.at[stage, way, self.sem],
+                recv_sem=recv_sem.at[stage, way, self.sem],
                 device_id={"dp": device},
                 device_id_type=pl.DeviceIdType.MESH,
             )
@@ -112,30 +112,52 @@
                 g_hbm.at[0, c // per_matrix, piece, lanes], g_buf.at[c % G_SLOTS, piece, :], g_sem.at[c % G_SLOTS, i]
             )
 
+    def product(n, c, tokens):
+        return lax.dot_general(
+            a_buf[n % 2, tokens, :], g_buf[c % G_SLOTS, tokens, :], (((0,), (0,)), ((), ())), preferred_element_type=f32
+        )
+
+    def start(copies):
+        for copy in copies:
+            copy.start()
+
+    def wait(copies):
+        for copy in copies:
+            copy.wait()
+
     def multiply(c):
         k = Chunk(c)
 
-        @pl.when(c % per_matrix == 0)
+        @pl.when(c == 0)
         def _():
-            for copy in a_copies(k.matrix):
-                copy.wait()
-
-            @pl.when(k.matrix + 1 < matrices)
+            depth = tokens // PIECES
+            pieces = list(zip(a_copies(0), g_copies(0)))
+            for i in range(PIECES):
+                wait(pieces[i])
+                if i + 2 < PIECES:
+                    start(pieces[i + 2])
+                elif i + 2 == PIECES:
+                    start(g_copies(1))
+                term = product(0, 0, slice(i * depth, (i + 1) * depth))
+                acc[0] = term if i == 0 else acc[0] + term
+
+        @pl.when(c > 0)
+        def _():
+            @pl.when(c % per_matrix == 0)
             def _():
-                for copy in a_copies(k.matrix + 1):
-                    copy.start()
-
-        for copy in g_copies(c):
-            copy.wait()
+                wait(a_copies(k.matrix))
+
+            wait(g_copies(c))
+            acc[c % 2] = product(k.matrix, c, slice(None))
+
+        @pl.when((c % per_matrix == 0) & (k.matrix + 1 < matrices))
+        def _():
+            start(a_copies(k.matrix + 1))
 
         @pl.when(c + 2 < chunks)
         def _():
-            for copy in g_copies(c + 2):
-                copy.start()
-
-        acc[c % 2] = lax.dot_general(
-            a_buf[k.matrix % 2], g_buf[c % G_SLOTS], (((0,), (0,)), ((), ())), preferred_element_type=f32
-        )
+            start(g_copies(c + 2))
+
         buf = send_bufs[0]
         buf[k.slot, 0, :half1] = k.term(2, 0).astype(bf16)
         buf[k.slot, 0, half1:] = k.term(1, 1).astype(bf16)
@@ -205,17 +227,16 @@
     def gathered1(c):
         Chunk(c).received(7)
 
-    sends = [0, 1, 2, 3, 4, 5, 6 + HOLD, 7 + HOLD]
-    steps = list(zip(sends, (multiply, relay1, shard1, relay2, shard2, gather2, gather1, relay_gather1)))
-    steps += [(6, gathered2), (8 + HOLD, gathered1)]
-    steps.sort(key=lambda step: step[0])
+    sends = [0, 1, 2, 3, 4, 5, 6, 9]
+    steps = list(zip(sends, (multiply, relay1, shard1, relay2, shard2, gather2)))
+    steps += [(6, gathered2), (sends[6], gather1), (sends[7], relay_gather1), (12, gathered1)]
     for stage, lag in enumerate(sends):
-        steps.append((lag + 2, functools.partial(lambda stage, c: Chunk(c).sent(stage), stage)))
+        steps.append((lag + 3, functools.partial(lambda stage, c: Chunk(c).sent(stage), stage)))
 
     barrier = pltpu.get_barrier_semaphore()
     here = Chunk(0)
-    for copy in (*a_copies(0), *g_copies(0), *g_copies(1)):
-        copy.start()
+    for pair in list(zip(a_copies(0), g_copies(0)))[:2]:
+        start(pair)
     for to in (1, -1):
         for device in (here.first(to), here.second(to)):
             pl.semaphore_signal(barrier, inc=1, device_id={"dp": device}, device_id_type=pl.DeviceIdType.MESH)
@@ -272,8 +293,8 @@
                 *messages,
                 pltpu.SemaphoreType.DMA((2, PIECES)),
                 pltpu.SemaphoreType.DMA((G_SLOTS, PIECES)),
-                pltpu.SemaphoreType.DMA((8, 2, SLOTS)),
-                pltpu.SemaphoreType.DMA((8, 2, SLOTS)),
+                pltpu.SemaphoreType.DMA((8, 2, SEMS)),
+                pltpu.SemaphoreType.DMA((8, 2, SEMS)),
             ],
             compiler_params=pltpu.CompilerParams(
                 collective_id=0, has_side_effects=True, vmem_limit_bytes=50 << 20

time: 175 us -> 163 us (0.931)
  Pallas kernels: 175 us -> 163 us
    pallas_call x1, Pallas kernels: 170 us -> 158 us  [body(): pl.pallas_call(functools.partial(kernel, side), name='gradient_sums', out...]
where the time goes in v3:
time: 163 us
  Pallas kernels  163 us (100%)
    pallas_call x1, Pallas kernels, body(): pl.pallas_call(functools.partial(kernel, side), name='gradient_sums', out...  158 us
    pallas_call x1, Pallas kernels, body(): pl.pallas_call(write, name='write_sums', out_shape=jax.ShapeDtypeStruct(s...  4.87 us

profile of v3, /device:TPU:96, one launch (start us, length us, event | category | flops | bytes accessed | tf_op | source)
XLA Modules:
  0.0 162.6 jit_solution(1641525759473295944)
XLA Ops:
  0.0 157.7 %gradient_sums.1.sums = bf16[4,640,2560]{2,1,0:T(8,128)(2,1)S(1)} custom-call(bf16[1,4,4096,640]{3,2,1,0:T(8,128)(2,1)} %a_hbm.1, bf16[1,4,4096,2560]{3,2,1,0:T(8,128)(2,1)} %g_hbm.1), custom_call_target="tpu_custom_call" | custom-call | tf_op jit(solution)/shard_map/gradient_sums/pallas_call | solution.py:280
  157.8 4.9 %write_sums.1 = bf16[4,640,2560]{2,1,0:T(8,128)(2,1)} custom-call(bf16[4,640,2560]{2,1,0:T(8,128)(2,1)S(1)} %gradient_sums.1.sums), custom_call_target="tpu_custom_call" | custom-call | tf_op jit(solution)/shard_map/write_sums/pallas_call | solution.py:303

commit v4 on v3

--- a/solution.py
+++ b/solution.py
@@ -9,8 +9,9 @@
 from jax.sharding import PartitionSpec as P
 
 LANES = 128
-SLOTS = 4
-SEMS = 8
+SEND_SLOTS = 4
+RECV_SLOTS = 8
+ACC_SLOTS = 4
 PIECES = 4
 G_SLOTS = 3
 
@@ -31,7 +32,7 @@
     class Chunk:
         def __init__(self, c):
             odd = (c + swap) % 2
-            self.c, self.slot, self.sem = c, c % SLOTS, c % SEMS
+            self.c, self.slot, self.recv = c, c % SEND_SLOTS, c % RECV_SLOTS
             self.matrix = c // per_matrix
             self.column = (c % per_matrix) * width
             self.p = x * (1 - odd) + y * odd
@@ -48,11 +49,11 @@
         def term(self, d, half):
             s = (self.p + d + side) % side
             lanes = pl.ds(pl.multiple_of(s * LANES, LANES), LANES)
-            return acc[self.c % 2, half * half1 : (half + 1) * half1, lanes]
+            return acc[self.c % ACC_SLOTS, half * half1 : (half + 1) * half1, lanes]
 
         def sub(self, d, half):
             s = (self.q + d + side) % side
-            return part[self.slot, pl.ds(pl.multiple_of(s * rows2 + half * half2, half2), half2), :]
+            return part[self.recv, pl.ds(pl.multiple_of(s * rows2 + half * half2, half2), half2), :]
 
         def block(self, d1, start, size):
             s = (self.p + d1 + side) % side
@@ -62,7 +63,7 @@
         def copy(self, stage, way):
             to = 1 - 2 * way
             if stage < 4:
-                src, dst = send_bufs[stage].at[self.slot, way], recv_bufs[stage].at[self.slot, way]
+                src, dst = send_bufs[stage].at[self.slot, way], recv_bufs[stage].at[self.recv, way]
                 device = self.first(to) if stage < 2 else self.second(to)
             elif stage == 4:
                 src = dst = self.block(0, self.q * rows2, rows2)
@@ -79,8 +80,8 @@
             return pltpu.make_async_remote_copy(
                 src_ref=src,
                 dst_ref=dst,
-                send_sem=send_sem.at[stage, way, self.sem],
-                recv_sem=recv_sem.at[stage, way, self.sem],
+                send_sem=send_sem.at[stage, way, self.recv],
+                recv_sem=recv_sem.at[stage, way, self.recv],
                 device_id={"dp": device},
                 device_id_type=pl.DeviceIdType.MESH,
             )
@@ -148,7 +149,7 @@
                 wait(a_copies(k.matrix))
 
             wait(g_copies(c))
-            acc[c % 2] = product(k.matrix, c, slice(None))
+            acc[c % ACC_SLOTS] = product(k.matrix, c, slice(None))
 
         @pl.when((c % per_matrix == 0) & (k.matrix + 1 < matrices))
         def _():
@@ -169,18 +170,18 @@
         k = Chunk(c)
         k.received(0)
         got, buf = recv_bufs[0], send_bufs[1]
-        buf[k.slot, 0] = (k.term(1, 0) + got[k.slot, 0, :half1].astype(f32)).astype(bf16)
-        buf[k.slot, 1] = (k.term(-1, 1) + got[k.slot, 1, half1:].astype(f32)).astype(bf16)
+        buf[k.slot, 0] = (k.term(1, 0) + got[k.recv, 0, :half1].astype(f32)).astype(bf16)
+        buf[k.slot, 1] = (k.term(-1, 1) + got[k.recv, 1, half1:].astype(f32)).astype(bf16)
         k.send(1)
-        part[k.slot, :half1] = k.term(0, 0) + got[k.slot, 1, :half1].astype(f32)
-        part[k.slot, half1:] = k.term(0, 1) + got[k.slot, 0, half1:].astype(f32)
+        part[k.recv, :half1] = k.term(0, 0) + got[k.recv, 1, :half1].astype(f32)
+        part[k.recv, half1:] = k.term(0, 1) + got[k.recv, 0, half1:].astype(f32)
 
     def shard1(c):
         k = Chunk(c)
         k.received(1)
         got = recv_bufs[1]
-        part[k.slot, :half1] += got[k.slot, 0].astype(f32)
-        part[k.slot, half1:] += got[k.slot, 1].astype(f32)
+        part[k.recv, :half1] += got[k.recv, 0].astype(f32)
+        part[k.recv, half1:] += got[k.recv, 1].astype(f32)
         buf = send_bufs[2]
         buf[k.slot, 0, :half2] = k.sub(2, 0).astype(bf16)
         buf[k.slot, 0, half2:] = k.sub(1, 1).astype(bf16)
@@ -192,18 +193,18 @@
         k = Chunk(c)
         k.received(2)
         got, buf = recv_bufs[2], send_bufs[3]
-        buf[k.slot, 0] = (k.sub(1, 0) + got[k.slot, 0, :half2].astype(f32)).astype(bf16)
-        buf[k.slot, 1] = (k.sub(-1, 1) + got[k.slot, 1, half2:].astype(f32)).astype(bf16)
+        buf[k.slot, 0] = (k.sub(1, 0) + got[k.recv, 0, :half2].astype(f32)).astype(bf16)
+        buf[k.slot, 1] = (k.sub(-1, 1) + got[k.recv, 1, half2:].astype(f32)).astype(bf16)
         k.send(3)
-        mine[k.slot, :half2] = k.sub(0, 0) + got[k.slot, 1, :half2].astype(f32)
-        mine[k.slot, half2:] = k.sub(0, 1) + got[k.slot, 0, half2:].astype(f32)
+        mine[k.slot, :half2] = k.sub(0, 0) + got[k.recv, 1, :half2].astype(f32)
+        mine[k.slot, half2:] = k.sub(0, 1) + got[k.recv, 0, half2:].astype(f32)
 
     def shard2(c):
         k = Chunk(c)
         k.received(3)
         got = recv_bufs[3]
-        low = mine[k.slot, :half2] + got[k.slot, 0].astype(f32)
-        high = mine[k.slot, half2:] + got[k.slot, 1].astype(f32)
+        low = mine[k.slot, :half2] + got[k.recv, 0].astype(f32)
+        high = mine[k.slot, half2:] + got[k.recv, 1].astype(f32)
         k.block(0, k.q * rows2, half2)[...] = low.astype(bf16)
         k.block(0, k.q * rows2 + half2, half2)[...] = high.astype(bf16)
         k.send(4)
@@ -227,9 +228,9 @@
     def gathered1(c):
         Chunk(c).received(7)
 
-    sends = [0, 1, 2, 3, 4, 5, 6, 9]
+    sends = [0, 2, 4, 6, 8, 10, 12, 15]
     steps = list(zip(sends, (multiply, relay1, shard1, relay2, shard2, gather2)))
-    steps += [(6, gathered2), (sends[6], gather1), (sends[7], relay_gather1), (12, gathered1)]
+    steps += [(12, gathered2), (sends[6], gather1), (sends[7], relay_gather1), (18, gathered1)]
     for stage, lag in enumerate(sends):
         steps.append((lag + 3, functools.partial(lambda stage, c: Chunk(c).sent(stage), stage)))
 
@@ -276,7 +277,9 @@
         columns = g.shape[3]
         width = side * LANES
         sizes = (rows, rows // 2, rows // side, rows // side // 2)
-        messages = [pltpu.VMEM((SLOTS, 2, size, LANES), jnp.bfloat16) for size in sizes]
+        messages = [
+            pltpu.VMEM((slots, 2, size, LANES), jnp.bfloat16) for slots in (SEND_SLOTS, RECV_SLOTS) for size in sizes
+        ]
         sums = pl.pallas_call(
             functools.partial(kernel, side),
             name="gradient_sums",
@@ -286,15 +289,14 @@
             scratch_shapes=[
                 pltpu.VMEM((2, tokens, rows), jnp.bfloat16),
                 pltpu.VMEM((G_SLOTS, tokens, width), jnp.bfloat16),
-                pltpu.VMEM((2, rows, width), jnp.float32),
-                pltpu.VMEM((SLOTS, rows, LANES), jnp.float32),
-                pltpu.VMEM((SLOTS, rows // side, LANES), jnp.float32),
-                *messages,
+                pltpu.VMEM((ACC_SLOTS, rows, width), jnp.float32),
+                pltpu.VMEM((RECV_SLOTS, rows, LANES), jnp.float32),
+                pltpu.VMEM((SEND_SLOTS, rows // side, LANES), jnp.float32),
                 *messages,
                 pltpu.SemaphoreType.DMA((2, PIECES)),
                 pltpu.SemaphoreType.DMA((G_SLOTS, PIECES)),
-                pltpu.SemaphoreType.DMA((8, 2, SEMS)),
-                pltpu.SemaphoreType.DMA((8, 2, SEMS)),
+                pltpu.SemaphoreType.DMA((8, 2, RECV_SLOTS)),
+                pltpu.SemaphoreType.DMA((8, 2, RECV_SLOTS)),
             ],
             compiler_params=pltpu.CompilerParams(
                 collective_id=0, has_side_effects=True, vmem_limit_bytes=50 << 20

time: 163 us -> 159 us (0.975)
  the two profiles are of different devices: /device:TPU:96 before, /device:TPU:97 now
where the time goes in v4:
time: 159 us; the launch traced here: 158 us
  Pallas kernels  158 us (99%)
    pallas_call x1, Pallas kernels, body(): pl.pallas_call(functools.partial(kernel, side), name='gradient_sums', out...  154 us
    pallas_call x1, Pallas kernels, body(): pl.pallas_call(write, name='write_sums', out_shape=jax.ShapeDtypeStruct(s...  4.87 us

profile of v4, /device:TPU:97, one launch (start us, length us, event | category | flops | bytes accessed | tf_op | source)
XLA Modules:
  0.0 158.4 jit_solution(3098175478122108596)
XLA Ops:
  0.0 153.5 %gradient_sums.1.sums = bf16[4,640,2560]{2,1,0:T(8,128)(2,1)S(1)} custom-call(bf16[1,4,4096,640]{3,2,1,0:T(8,128)(2,1)} %a_hbm.1, bf16[1,4,4096,2560]{3,2,1,0:T(8,128)(2,1)} %g_hbm.1), custom_call_target="tpu_custom_call" | custom-call | tf_op jit(solution)/shard_map/gradient_sums/pallas_call | solution.py:283
  153.6 4.9 %write_sums.1 = bf16[4,640,2560]{2,1,0:T(8,128)(2,1)} custom-call(bf16[4,640,2560]{2,1,0:T(8,128)(2,1)S(1)} %gradient_sums.1.sums), custom_call_target="tpu_custom_call" | custom-call | tf_op jit(solution)/shard_map/write_sums/pallas_call | solution.py:305

commit v5 on v4

--- a/solution.py
+++ b/solution.py
@@ -11,12 +11,11 @@
 LANES = 128
 SEND_SLOTS = 4
 RECV_SLOTS = 8
-ACC_SLOTS = 4
 PIECES = 4
 G_SLOTS = 3
 
 
-def kernel(side, a_hbm, g_hbm, out, a_buf, g_buf, acc, part, mine, *rest):
+def kernel(side, a_hbm, g_hbm, out, a_buf, g_buf, total, acc, part, mine, *rest):
     send_bufs, recv_bufs = rest[:4], rest[4:8]
     a_sem, g_sem, send_sem, recv_sem = rest[8:]
     matrices, tokens, rows = a_hbm.shape[1:]
@@ -34,7 +33,7 @@
             odd = (c + swap) % 2
             self.c, self.slot, self.recv = c, c % SEND_SLOTS, c % RECV_SLOTS
             self.matrix = c // per_matrix
-            self.column = (c % per_matrix) * width
+            self.column = (c % per_matrix) * side
             self.p = x * (1 - odd) + y * odd
             self.q = y * (1 - odd) + x * odd
             self.stride1 = side * (1 - odd) + odd
@@ -46,10 +45,8 @@
         def second(self, d):
             return self.p * self.stride1 + (self.q + d + side) % side * self.stride2
 
-        def term(self, d, half):
-            s = (self.p + d + side) % side
-            lanes = pl.ds(pl.multiple_of(s * LANES, LANES), LANES)
-            return acc[self.c % ACC_SLOTS, half * half1 : (half + 1) * half1, lanes]
+        def lanes(self, d):
+            return pl.ds(pl.multiple_of((self.p + d + side) % side * LANES, LANES), LANES)
 
         def sub(self, d, half):
             s = (self.q + d + side) % side
@@ -57,8 +54,7 @@
 
         def block(self, d1, start, size):
             s = (self.p + d1 + side) % side
-            lanes = pl.ds(pl.multiple_of(self.column + s * LANES, LANES), LANES)
-            return out.at[self.matrix, pl.ds(pl.multiple_of(start, 16), size), lanes]
+            return out.at[self.matrix, self.column + s, pl.ds(pl.multiple_of(start, 16), size), :]
 
         def copy(self, stage, way):
             to = 1 - 2 * way
@@ -113,10 +109,23 @@
                 g_hbm.at[0, c // per_matrix, piece, lanes], g_buf.at[c % G_SLOTS, piece, :], g_sem.at[c % G_SLOTS, i]
             )
 
-    def product(n, c, tokens):
+    def product(k, tokens):
+        g = g_buf.at[k.c % G_SLOTS]
+        columns = jnp.concatenate([g[tokens, k.lanes(d)] for d in (1, 2, -1, 0)], axis=1)
         return lax.dot_general(
-            a_buf[n % 2, tokens, :], g_buf[c % G_SLOTS, tokens, :], (((0,), (0,)), ((), ())), preferred_element_type=f32
+            a_buf[k.matrix % 2, tokens, :], columns, (((0,), (0,)), ((), ())), preferred_element_type=f32
         )
+
+    def store(k, product):
+        right, far, left, own = (product[:, i * LANES : (i + 1) * LANES] for i in range(4))
+        buf = send_bufs[0]
+        buf[k.slot, 0, :half1] = far[:half1].astype(bf16)
+        buf[k.slot, 0, half1:] = right[half1:].astype(bf16)
+        buf[k.slot, 1, :half1] = left[:half1].astype(bf16)
+        buf[k.slot, 1, half1:] = far[half1:].astype(bf16)
+        acc[k.slot, 0] = right[:half1]
+        acc[k.slot, 1] = left[half1:]
+        part[k.recv] = own
 
     def start(copies):
         for copy in copies:
@@ -139,8 +148,13 @@
                     start(pieces[i + 2])
                 elif i + 2 == PIECES:
                     start(g_copies(1))
-                term = product(0, 0, slice(i * depth, (i + 1) * depth))
-                acc[0] = term if i == 0 else acc[0] + term
+                term = product(k, slice(i * depth, (i + 1) * depth))
+                if i == 0:
+                    total[...] = term
+                elif i + 1 < PIECES:
+                    total[...] += term
+                else:
+                    store(k, total[...] + term)
 
         @pl.when(c > 0)
         def _():
@@ -149,7 +163,7 @@
                 wait(a_copies(k.matrix))
 
             wait(g_copies(c))
-            acc[c % ACC_SLOTS] = product(k.matrix, c, slice(None))
+            store(k, product(k, slice(None)))
 
         @pl.when((c % per_matrix == 0) & (k.matrix + 1 < matrices))
         def _():
@@ -159,22 +173,17 @@
         def _():
             start(g_copies(c + 2))
 
-        buf = send_bufs[0]
-        buf[k.slot, 0, :half1] = k.term(2, 0).astype(bf16)
-        buf[k.slot, 0, half1:] = k.term(1, 1).astype(bf16)
-        buf[k.slot, 1, :half1] = k.term(-1, 0).astype(bf16)
-        buf[k.slot, 1, half1:] = k.term(2, 1).astype(bf16)
         k.send(0)
 
     def relay1(c):
         k = Chunk(c)
         k.received(0)
         got, buf = recv_bufs[0], send_bufs[1]
-        buf[k.slot, 0] = (k.term(1, 0) + got[k.recv, 0, :half1].astype(f32)).astype(bf16)
-        buf[k.slot, 1] = (k.term(-1, 1) + got[k.recv, 1, half1:].astype(f32)).astype(bf16)
+        buf[k.slot, 0] = (acc[k.slot, 0] + got[k.recv, 0, :half1].astype(f32)).astype(bf16)
+        buf[k.slot, 1] = (acc[k.slot, 1] + got[k.recv, 1, half1:].astype(f32)).astype(bf16)
         k.send(1)
-        part[k.recv, :half1] = k.term(0, 0) + got[k.recv, 1, :half1].astype(f32)
-        part[k.recv, half1:] = k.term(0, 1) + got[k.recv, 0, half1:].astype(f32)
+        part[k.recv, :half1] += got[k.recv, 1, :half1].astype(f32)
+        part[k.recv, half1:] += got[k.recv, 0, half1:].astype(f32)
 
     def shard1(c):
         k = Chunk(c)
@@ -254,14 +263,11 @@
 
 
 def write(sums, out, sem):
-    matrices, rows = sums.shape[:2]
-    size = rows // PIECES
+    matrices, blocks = sums.shape[:2]
     copies = [
-        pltpu.make_async_copy(
-            sums.at[n, i * size : (i + 1) * size], out.at[n, i * size : (i + 1) * size], sem.at[n, i]
-        )
+        pltpu.make_async_copy(sums.at[n, i], out.at[n, :, i * LANES : (i + 1) * LANES], sem.at[n, i])
         for n in range(matrices)
-        for i in range(PIECES)
+        for i in range(blocks)
     ]
     for copy in copies:
         copy.start()
@@ -283,13 +289,14 @@
         sums = pl.pallas_call(
             functools.partial(kernel, side),
             name="gradient_sums",
-            out_shape=pltpu.VMEM((matrices, rows, columns), jnp.bfloat16),
+            out_shape=pltpu.VMEM((matrices, columns // LANES, rows, LANES), jnp.bfloat16),
             in_specs=[pl.BlockSpec(memory_space=pl.ANY)] * 2,
             out_specs=pl.BlockSpec(memory_space=pltpu.VMEM),
             scratch_shapes=[
                 pltpu.VMEM((2, tokens, rows), jnp.bfloat16),
                 pltpu.VMEM((G_SLOTS, tokens, width), jnp.bfloat16),
-                pltpu.VMEM((ACC_SLOTS, rows, width), jnp.float32),
+                pltpu.VMEM((rows, width), jnp.float32),
+                pltpu.VMEM((SEND_SLOTS, 2, rows // 2, LANES), jnp.float32),
                 pltpu.VMEM((RECV_SLOTS, rows, LANES), jnp.float32),
                 pltpu.VMEM((SEND_SLOTS, rows // side, LANES), jnp.float32),
                 *messages,
@@ -305,10 +312,10 @@
         return pl.pallas_call(
             write,
             name="write_sums",
-            out_shape=jax.ShapeDtypeStruct(sums.shape, sums.dtype),
+            out_shape=jax.ShapeDtypeStruct((matrices, rows, columns), sums.dtype),
             in_specs=[pl.BlockSpec(memory_space=pltpu.VMEM)],
             out_specs=pl.BlockSpec(memory_space=pl.ANY),
-            scratch_shapes=[pltpu.SemaphoreType.DMA((matrices, PIECES))],
+            scratch_shapes=[pltpu.SemaphoreType.DMA((matrices, columns // LANES))],
             compiler_params=pltpu.CompilerParams(vmem_limit_bytes=1 << 20),
         )(sums)
 

time: 159 us -> 158 us (level)
  no operation moved by 1% of the time
where the time goes in v5:
time: 158 us
  Pallas kernels  158 us (100%)
    pallas_call x1, Pallas kernels, body(): pl.pallas_call(functools.partial(kernel, side), name='gradient_sums', out...  153 us
    pallas_call x1, Pallas kernels, body(): pl.pallas_call(write, name='write_sums', out_shape=jax.ShapeDtypeStruct((...  5.37 us

profile of v5, /device:TPU:97, one launch (start us, length us, event | category | flops | bytes accessed | tf_op | source)
XLA Modules:
  0.0 158.0 jit_solution(18262566153061459641)
XLA Ops:
  0.0 152.6 %gradient_sums.1.sums = bf16[4,20,640,128]{3,2,1,0:T(8,128)(2,1)S(1)} custom-call(bf16[1,4,4096,640]{3,2,1,0:T(8,128)(2,1)} %a_hbm.1, bf16[1,4,4096,2560]{3,2,1,0:T(8,128)(2,1)} %g_hbm.1), custom_call_target="tpu_custom_call" | custom-call | tf_op jit(solution)/shard_map/gradient_sums/pallas_call | solution.py:289
  152.6 5.4 %write_sums.1 = bf16[4,640,2560]{2,1,0:T(8,128)(2,1)} custom-call(bf16[4,20,640,128]{3,2,1,0:T(8,128)(2,1)S(1)} %gradient_sums.1.sums), custom_call_target="tpu_custom_call" | custom-call | tf_op jit(solution)/shard_map/write_sums/pallas_call | solution.py:312

commit v6 on v5

--- a/solution.py
+++ b/solution.py
@@ -11,7 +11,8 @@
 LANES = 128
 SEND_SLOTS = 4
 RECV_SLOTS = 8
-PIECES = 4
+PIECES = (0, 2, 6, 11, 16)
+WRITES = 4
 G_SLOTS = 3
 
 
@@ -26,6 +27,7 @@
     half2 = rows2 // 2
     me, swap = lax.axis_index("dp"), lax.axis_index("rep") % 2
     x, y = me // side, me % side
+    barrier = pltpu.get_barrier_semaphore()
     bf16, f32 = jnp.bfloat16, jnp.float32
 
     class Chunk:
@@ -33,7 +35,7 @@
             odd = (c + swap) % 2
             self.c, self.slot, self.recv = c, c % SEND_SLOTS, c % RECV_SLOTS
             self.matrix = c // per_matrix
-            self.column = (c % per_matrix) * side
+            self.column = (c % per_matrix) * width
             self.p = x * (1 - odd) + y * odd
             self.q = y * (1 - odd) + x * odd
             self.stride1 = side * (1 - odd) + odd
@@ -54,7 +56,8 @@
 
         def block(self, d1, start, size):
             s = (self.p + d1 + side) % side
-            return out.at[self.matrix, self.column + s, pl.ds(pl.multiple_of(start, 16), size), :]
+            lanes = pl.ds(pl.multiple_of(self.column + s * LANES, LANES), LANES)
+            return out.at[self.matrix, pl.ds(pl.multiple_of(start, 16), size), lanes]
 
         def copy(self, stage, way):
             to = 1 - 2 * way
@@ -94,17 +97,15 @@
             for way in range(2):
                 self.copy(stage, way).wait_send()
 
+    pieces = [slice(i * tokens // 16, j * tokens // 16) for i, j in zip(PIECES, PIECES[1:])]
+
     def a_copies(n):
-        depth = tokens // PIECES
-        for i in range(PIECES):
-            piece = pl.ds(i * depth, depth)
+        for i, piece in enumerate(pieces):
             yield pltpu.make_async_copy(a_hbm.at[0, n, piece, :], a_buf.at[n % 2, piece, :], a_sem.at[n % 2, i])
 
     def g_copies(c):
-        depth = tokens // PIECES
         lanes = pl.ds(pl.multiple_of(c % per_matrix * width, width), width)
-        for i in range(PIECES):
-            piece = pl.ds(i * depth, depth)
+        for i, piece in enumerate(pieces):
             yield pltpu.make_async_copy(
                 g_hbm.at[0, c // per_matrix, piece, lanes], g_buf.at[c % G_SLOTS, piece, :], g_sem.at[c % G_SLOTS, i]
             )
@@ -140,21 +141,21 @@
 
         @pl.when(c == 0)
         def _():
-            depth = tokens // PIECES
-            pieces = list(zip(a_copies(0), g_copies(0)))
-            for i in range(PIECES):
-                wait(pieces[i])
-                if i + 2 < PIECES:
-                    start(pieces[i + 2])
-                elif i + 2 == PIECES:
+            copies = list(zip(a_copies(0), g_copies(0)))
+            for i, piece in enumerate(pieces):
+                wait(copies[i])
+                if i + 2 < len(pieces):
+                    start(copies[i + 2])
+                elif i + 2 == len(pieces):
                     start(g_copies(1))
-                term = product(k, slice(i * depth, (i + 1) * depth))
+                term = product(k, piece)
                 if i == 0:
                     total[...] = term
-                elif i + 1 < PIECES:
+                elif i + 1 < len(pieces):
                     total[...] += term
                 else:
                     store(k, total[...] + term)
+            pl.semaphore_wait(barrier, 4)
 
         @pl.when(c > 0)
         def _():
@@ -243,14 +244,12 @@
     for stage, lag in enumerate(sends):
         steps.append((lag + 3, functools.partial(lambda stage, c: Chunk(c).sent(stage), stage)))
 
-    barrier = pltpu.get_barrier_semaphore()
     here = Chunk(0)
     for pair in list(zip(a_copies(0), g_copies(0)))[:2]:
         start(pair)
     for to in (1, -1):
         for device in (here.first(to), here.second(to)):
             pl.semaphore_signal(barrier, inc=1, device_id={"dp": device}, device_id_type=pl.DeviceIdType.MESH)
-    pl.semaphore_wait(barrier, 4)
 
     def turn(t, carry):
         for lag, do in steps:
@@ -263,11 +262,14 @@
 
 
 def write(sums, out, sem):
-    matrices, blocks = sums.shape[:2]
+    matrices, rows = sums.shape[:2]
+    size = rows // WRITES
     copies = [
-        pltpu.make_async_copy(sums.at[n, i], out.at[n, :, i * LANES : (i + 1) * LANES], sem.at[n, i])
+        pltpu.make_async_copy(
+            sums.at[n, i * size : (i + 1) * size], out.at[n, i * size : (i + 1) * size], sem.at[n, i]
+        )
         for n in range(matrices)
-        for i in range(blocks)
+        for i in range(WRITES)
     ]
     for copy in copies:
         copy.start()
@@ -289,7 +291,7 @@
         sums = pl.pallas_call(
             functools.partial(kernel, side),
             name="gradient_sums",
-            out_shape=pltpu.VMEM((matrices, columns // LANES, rows, LANES), jnp.bfloat16),
+            out_shape=pltpu.VMEM((matrices, rows, columns), jnp.bfloat16),
             in_specs=[pl.BlockSpec(memory_space=pl.ANY)] * 2,
             out_specs=pl.BlockSpec(memory_space=pltpu.VMEM),
             scratch_shapes=[
@@ -300,8 +302,8 @@
                 pltpu.VMEM((RECV_SLOTS, rows, LANES), jnp.float32),
                 pltpu.VMEM((SEND_SLOTS, rows // side, LANES), jnp.float32),
                 *messages,
-                pltpu.SemaphoreType.DMA((2, PIECES)),
-                pltpu.SemaphoreType.DMA((G_SLOTS, PIECES)),
+                pltpu.SemaphoreType.DMA((2, len(PIECES) - 1)),
+                pltpu.SemaphoreType.DMA((G_SLOTS, len(PIECES) - 1)),
                 pltpu.SemaphoreType.DMA((8, 2, RECV_SLOTS)),
                 pltpu.SemaphoreType.DMA((8, 2, RECV_SLOTS)),
             ],
@@ -312,10 +314,10 @@
         return pl.pallas_call(
             write,
             name="write_sums",
-            out_shape=jax.ShapeDtypeStruct((matrices, rows, columns), sums.dtype),
+            out_shape=jax.ShapeDtypeStruct(sums.shape, sums.dtype),
             in_specs=[pl.BlockSpec(memory_space=pltpu.VMEM)],
             out_specs=pl.BlockSpec(memory_space=pl.ANY),
-            scratch_shapes=[pltpu.SemaphoreType.DMA((matrices, columns // LANES))],
+            scratch_shapes=[pltpu.SemaphoreType.DMA((matrices, WRITES))],
             compiler_params=pltpu.CompilerParams(vmem_limit_bytes=1 << 20),
         )(sums)
 

time: 158 us -> 157 us (level)
  no operation moved by 1% of the time
where the time goes in v6:
time: 157 us
  Pallas kernels  157 us (100%)
    pallas_call x1, Pallas kernels, body(): pl.pallas_call(functools.partial(kernel, side), name='gradient_sums', out...  153 us
    pallas_call x1, Pallas kernels, body(): pl.pallas_call(write, name='write_sums', out_shape=jax.ShapeDtypeStruct(s...  4.87 us

profile of v6, /device:TPU:97, one launch (start us, length us, event | category | flops | bytes accessed | tf_op | source)
XLA Modules:
  0.0 157.4 jit_solution(8844522039073667333)
XLA Ops:
  0.0 152.5 %gradient_sums.1.sums = bf16[4,640,2560]{2,1,0:T(8,128)(2,1)S(1)} custom-call(bf16[1,4,4096,640]{3,2,1,0:T(8,128)(2,1)} %a_hbm.1, bf16[1,4,4096,2560]{3,2,1,0:T(8,128)(2,1)} %g_hbm.1), custom_call_target="tpu_custom_call" | custom-call | tf_op jit(solution)/shard_map/gradient_sums/pallas_call | solution.py:291
  152.5 4.9 %write_sums.1 = bf16[4,640,2560]{2,1,0:T(8,128)(2,1)} custom-call(bf16[4,640,2560]{2,1,0:T(8,128)(2,1)S(1)} %gradient_sums.1.sums), custom_call_target="tpu_custom_call" | custom-call | tf_op jit(solution)/shard_map/write_sums/pallas_call | solution.py:314

commit v7 on v6

--- a/solution.py
+++ b/solution.py
@@ -11,6 +11,7 @@
 LANES = 128
 SEND_SLOTS = 4
 RECV_SLOTS = 8
+SEM_SLOTS = 12
 PIECES = (0, 2, 6, 11, 16)
 WRITES = 4
 G_SLOTS = 3
@@ -33,7 +34,7 @@
     class Chunk:
         def __init__(self, c):
             odd = (c + swap) % 2
-            self.c, self.slot, self.recv = c, c % SEND_SLOTS, c % RECV_SLOTS
+            self.c, self.slot, self.recv, self.sem = c, c % SEND_SLOTS, c % RECV_SLOTS, c % SEM_SLOTS
             self.matrix = c // per_matrix
             self.column = (c % per_matrix) * width
             self.p = x * (1 - odd) + y * odd
@@ -79,8 +80,8 @@
             return pltpu.make_async_remote_copy(
                 src_ref=src,
                 dst_ref=dst,
-                send_sem=send_sem.at[stage, way, self.recv],
-                recv_sem=recv_sem.at[stage, way, self.recv],
+                send_sem=send_sem.at[stage, way, self.sem],
+                recv_sem=recv_sem.at[stage, way, self.sem],
                 device_id={"dp": device},
                 device_id_type=pl.DeviceIdType.MESH,
             )
@@ -238,9 +239,9 @@
     def gathered1(c):
         Chunk(c).received(7)
 
-    sends = [0, 2, 4, 6, 8, 10, 12, 15]
+    sends = [0, 2, 4, 6, 8, 10, 12, 17]
     steps = list(zip(sends, (multiply, relay1, shard1, relay2, shard2, gather2)))
-    steps += [(12, gathered2), (sends[6], gather1), (sends[7], relay_gather1), (18, gathered1)]
+    steps += [(12, gathered2), (sends[6], gather1), (sends[7], relay_gather1), (22, gathered1)]
     for stage, lag in enumerate(sends):
         steps.append((lag + 3, functools.partial(lambda stage, c: Chunk(c).sent(stage), stage)))
 
@@ -304,8 +305,8 @@
                 *messages,
                 pltpu.SemaphoreType.DMA((2, len(PIECES) - 1)),
                 pltpu.SemaphoreType.DMA((G_SLOTS, len(PIECES) - 1)),
-                pltpu.SemaphoreType.DMA((8, 2, RECV_SLOTS)),
-                pltpu.SemaphoreType.DMA((8, 2, RECV_SLOTS)),
+                pltpu.SemaphoreType.DMA((8, 2, SEM_SLOTS)),
+                pltpu.SemaphoreType.DMA((8, 2, SEM_SLOTS)),
             ],
             compiler_params=pltpu.CompilerParams(
                 collective_id=0, has_side_effects=True, vmem_limit_bytes=50 << 20

time: 157 us -> 158 us (level)
  no operation moved by 1% of the time
where the time goes in v7:
time: 158 us
  Pallas kernels  158 us (100%)
    pallas_call x1, Pallas kernels, body(): pl.pallas_call(functools.partial(kernel, side), name='gradient_sums', out...  153 us
    pallas_call x1, Pallas kernels, body(): pl.pallas_call(write, name='write_sums', out_shape=jax.ShapeDtypeStruct(s...  4.87 us

profile of v7, /device:TPU:97, one launch (start us, length us, event | category | flops | bytes accessed | tf_op | source)
XLA Modules:
  0.0 158.0 jit_solution(2418317240177972880)
XLA Ops:
  0.0 153.1 %gradient_sums.1.sums = bf16[4,640,2560]{2,1,0:T(8,128)(2,1)S(1)} custom-call(bf16[1,4,4096,640]{3,2,1,0:T(8,128)(2,1)} %a_hbm.1, bf16[1,4,4096,2560]{3,2,1,0:T(8,128)(2,1)} %g_hbm.1), custom_call_target="tpu_custom_call" | custom-call | tf_op jit(solution)/shard_map/gradient_sums/pallas_call | solution.py:292
  153.1 4.9 %write_sums.1 = bf16[4,640,2560]{2,1,0:T(8,128)(2,1)} custom-call(bf16[4,640,2560]{2,1,0:T(8,128)(2,1)S(1)} %gradient_sums.1.sums), custom_call_target="tpu_custom_call" | custom-call | tf_op jit(solution)/shard_map/write_sums/pallas_call | solution.py:315

commit v8 on v6

--- a/solution.py
+++ b/solution.py
@@ -12,7 +12,7 @@
 SEND_SLOTS = 4
 RECV_SLOTS = 8
 PIECES = (0, 2, 6, 11, 16)
-WRITES = 4
+WRITES = 8
 G_SLOTS = 3
 
 
@@ -238,9 +238,9 @@
     def gathered1(c):
         Chunk(c).received(7)
 
-    sends = [0, 2, 4, 6, 8, 10, 12, 15]
+    sends = [0, 2, 4, 6, 8, 10, 12, 14]
     steps = list(zip(sends, (multiply, relay1, shard1, relay2, shard2, gather2)))
-    steps += [(12, gathered2), (sends[6], gather1), (sends[7], relay_gather1), (18, gathered1)]
+    steps += [(12, gathered2), (sends[6], gather1), (sends[7], relay_gather1), (16, gathered1)]
     for stage, lag in enumerate(sends):
         steps.append((lag + 3, functools.partial(lambda stage, c: Chunk(c).sent(stage), stage)))
 

time: 157 us -> 158 us (level)
  no operation moved by 1% of the time
where the time goes in v8:
time: 158 us; the launch traced here: 157 us
  Pallas kernels  157 us (99%)
    pallas_call x1, Pallas kernels, body(): pl.pallas_call(functools.partial(kernel, side), name='gradient_sums', out...  152 us
    pallas_call x1, Pallas kernels, body(): pl.pallas_call(write, name='write_sums', out_shape=jax.ShapeDtypeStruct(s...  4.99 us

profile of v8, /device:TPU:97, one launch (start us, length us, event | category | flops | bytes accessed | tf_op | source)
XLA Modules:
  0.0 157.3 jit_solution(11937164823063133388)
XLA Ops:
  0.0 152.3 %gradient_sums.1.sums = bf16[4,640,2560]{2,1,0:T(8,128)(2,1)S(1)} custom-call(bf16[1,4,4096,640]{3,2,1,0:T(8,128)(2,1)} %a_hbm.1, bf16[1,4,4096,2560]{3,2,1,0:T(8,128)(2,1)} %g_hbm.1), custom_call_target="tpu_custom_call" | custom-call | tf_op jit(solution)/shard_map/gradient_sums/pallas_call | solution.py:291
  152.3 5.0 %write_sums.1 = bf16[4,640,2560]{2,1,0:T(8,128)(2,1)} custom-call(bf16[4,640,2560]{2,1,0:T(8,128)(2,1)S(1)} %gradient_sums.1.sums), custom_call_target="tpu_custom_call" | custom-call | tf_op jit(solution)/shard_map/write_sums/pallas_call | solution.py:314
